TPU v7x, 32 devices: a whole 2x2x4 slice. The times are simulated.
32 devices in a mesh: north: 8 (over y, x, core), deep: 4 (over z).
Axes of the slice: x: 2, y: 2, z: 4, core: 2. Of those that a mesh axis runs over, the one named last changes fastest.
Arguments:
- forcing: float32 [2, 128, 128, 256], P(None, None, 'north', 'deep'), may hold values from -6 to 6
- symbol_x: float32 [128], replicated, may hold values from 0.3 to 3
- symbol_y: float32 [128], replicated, may hold values from 0.3 to 3
- symbol_z: float32 [256], replicated, may hold values from 0.3 to 3
Outputs:
- coefficients: float32 [2, 128, 128, 256], P(None, 'north', 'deep')
All inputs are finite; a program needn't handle non-finite values.
Results may differ from a plain program's by a relative error of at most 0.000084.
Values sent between devices are 32-bit elements; how exact they have to be, the bound alone decides.
A program may use at most 64 MiB of HBM per device.

v0:
```python
import jax
import jax.numpy as jnp
from jax import lax
from jax.sharding import PartitionSpec as P


def transform_table(count):
    rank = jnp.arange(count)
    angle = (
        jnp.pi
        / (4 * count)
        * ((2 * rank[:, None] + 1) * (2 * rank[None, :] + 1) % (8 * count)).astype(jnp.float32)
    )
    return jnp.cos(angle) * (2.0 / count) ** 0.5


def to_modes(values, dim):
    moved = jnp.tensordot(
        values,
        transform_table(values.shape[dim]),
        axes=([dim], [0]),
        precision=lax.Precision.HIGHEST,
    )
    return jnp.moveaxis(moved, -1, dim)


def local(forcing, symbol_x, symbol_y, symbol_z):

    def line_step(part_values):
        part_values = to_modes(part_values, 1)
        part_values = lax.all_to_all(part_values, "north", split_axis=1, concat_axis=2, tiled=True)
        part_values = to_modes(part_values, 2)
        return part_values

    middle_cut = forcing.shape[0] // 2
    lower_part = line_step(lax.slice_in_dim(forcing, 0, middle_cut, axis=0))
    upper_part = line_step(lax.slice_in_dim(forcing, middle_cut, forcing.shape[0], axis=0))
    local_values = jnp.concatenate([lower_part, upper_part], axis=0)
    local_values = lax.all_to_all(local_values, "deep", split_axis=2, concat_axis=3, tiled=True)
    local_values = to_modes(local_values, 3)
    share_x = local_values.shape[1]
    part_x = lax.dynamic_slice_in_dim(symbol_x, lax.axis_index("north") * share_x, share_x)
    share_y = local_values.shape[2]
    part_y = lax.dynamic_slice_in_dim(symbol_y, lax.axis_index("deep") * share_y, share_y)
    symbol = part_x[:, None, None] + part_y[None, :, None] + symbol_z[None, None, :]
    local_values = local_values * ((1.0 - 0.2 * symbol) / (1.0 + 0.2 * symbol))
    return local_values


def solution(mesh):
    placed = (P(None, None, "north", "deep"), P(), P(), P())
    return jax.shard_map(
        local, mesh=mesh, in_specs=placed, out_specs=P(None, "north", "deep", None), check_vma=False
    )
```

profile of v0, /device:TPU:0, one launch (start us, length us, event | category | flops | bytes accessed | tf_op | source)
XLA Modules:
  0.0 82.2 jit_solution(1717362456120942008)
XLA Ops:
  0.0 1.3 %fusion.55 = (f32[1,128,16,64]{1,3,2,0:T(8,128)S(1)}, f32[1,128,16,64]{1,3,2,0:T(8,128)S(1)}) fusion(f32[2,128,16,64]{1,3,2,0:T(8,128)} %param.4), kind=kLoop, calls=%fused_computation.68 | loop fusion | bytes 2097152 | tf_op jit(solution)/shard_map/slice | solution.py:36
  1.3 0.9 %fusion.28 = f32[128,1024]{0,1:S(1)} fusion(f32[128,1024]{0,1:T(8,128)S(1)} %bitcast.71, s32[128]{0:T(128)S(1)} %multiply_add_fusion.1), kind=kOutput, calls=%fused_computation.39 | convolution fusion | flops 201572352 | bytes 1049088
  2.2 0.5 copy.16
  2.7 1.4 %reshape.96 = f32[8,1,16384]{2,1,0:T(1,128)} reshape(f32[128,1,16,64]{3,2,1,0:T(8,128)S(1)} %bitcast.62) | data formatting | bytes 1048576
  4.1 5.2 %all-to-all-start = ((f32[8,1,16384]{2,1,0:T(1,128)}), f32[8,1,16384]{2,1,0:T(1,128)S(1)}, u32[]{:S(2)}, u32[]{:S(2)}) async-start(f32[8,1,16384]{2,1,0:T(1,128)} %reshape.96), calls=%async_computation | async-start | bytes 1048576 | tf_op jit(solution)/shard_map/all_to_all | solution.py:31
  9.3 0.9 %fusion.25 = f32[128,1024]{0,1:S(1)} fusion(f32[128,1024]{0,1:T(8,128)S(1)} %bitcast.70, s32[128]{0:T(128)S(1)} %multiply_add_fusion.1), kind=kOutput, calls=%fused_computation.38 | convolution fusion | flops 201572352 | bytes 1049088
  10.2 0.5 copy.19
  10.7 1.4 %reshape.94 = f32[8,1,16384]{2,1,0:T(1,128)} reshape(f32[128,1,16,64]{3,2,1,0:T(8,128)S(1)} %bitcast.63) | data formatting | bytes 1048576
  12.2 6.9 %all-to-all-done = f32[8,1,16384]{2,1,0:T(1,128)S(1)} async-done(((f32[8,1,16384]{2,1,0:T(1,128)}), f32[8,1,16384]{2,1,0:T(1,128)S(1)}, u32[]{:S(2)}, u32[]{:S(2)}) %all-to-all-start) | async-done | bytes 524320 | tf_op jit(solution)/shard_map/all_to_all | solution.py:31
  19.0 3.7 %all-to-all-start.1 = ((f32[8,1,16384]{2,1,0:T(1,128)}), f32[8,1,16384]{2,1,0:T(1,128)S(1)}, u32[]{:S(2)}, u32[]{:S(2)}) async-start(f32[8,1,16384]{2,1,0:T(1,128)} %reshape.94), calls=%async_computation.1 | async-start | bytes 1048576 | tf_op jit(solution)/shard_map/all_to_all | solution.py:31
  22.7 0.6 broadcast.162
  23.3 1.9 %reduce.1 = f32[8,16384]{1,0:T(8,128)S(1)} reduce(f32[8,1,16384]{2,1,0:T(1,128)S(1)} %all-to-all-done, f32[]{:T(128)} %broadcast.162), dimensions={1}, to_apply=%all_to_all.35.reduce_sub_computation | reduce | bytes 1048580 | tf_op jit(solution)/shard_map/all_to_all | solution.py:31
  25.2 0.4 reshape.97
  25.6 0.1 copy.17
  25.7 1.9 %convolution_bitcast_fusion.1 = f32[1,16,128,64]{2,3,1,0:T(8,128)S(1)} fusion(f32[16,128,64]{2,1,0:T(8,128)S(1)} %bitcast.66, s32[128]{0:T(128)S(1)} %multiply_add_fusion.1), kind=kOutput, calls=%fused_computation.2 | convolution fusion | flops 201572352 | bytes 1049088 | tf_op jit(solution)/shard_map/dot_general | solution.py:18
  27.7 4.5 %all-to-all-done.1 = f32[8,1,16384]{2,1,0:T(1,128)S(1)} async-done(((f32[8,1,16384]{2,1,0:T(1,128)}), f32[8,1,16384]{2,1,0:T(1,128)S(1)}, u32[]{:S(2)}, u32[]{:S(2)}) %all-to-all-start.1) | async-done | bytes 524320 | tf_op jit(solution)/shard_map/all_to_all | solution.py:31
  32.2 1.9 %reduce = f32[8,16384]{1,0:T(8,128)S(1)} reduce(f32[8,1,16384]{2,1,0:T(1,128)S(1)} %all-to-all-done.1, f32[]{:T(128)} %broadcast.162), dimensions={1}, to_apply=%all_to_all.38.reduce_sub_computation | reduce | bytes 1048580 | tf_op jit(solution)/shard_map/all_to_all | solution.py:31
  34.1 0.4 reshape.95
  34.5 0.1 copy.20
  34.6 1.9 %convolution_bitcast_fusion = f32[1,16,128,64]{2,3,1,0:T(8,128)S(1)} fusion(f32[16,128,64]{2,1,0:T(8,128)S(1)} %bitcast.64, s32[128]{0:T(128)S(1)} %multiply_add_fusion.1), kind=kOutput, calls=%fused_computation.1 | convolution fusion | flops 201572352 | bytes 1049088 | tf_op jit(solution)/shard_map/dot_general | solution.py:18
  36.5 0.1 pad_maximum_fusion
  36.6 1.8 %copy.22 = f32[2,16,128,64]{3,1,0,2:T(8,128)S(1)} copy(f32[2,16,128,64]{2,3,1,0:T(8,128)S(1)} %pad_maximum_fusion) | data formatting | bytes 2097152 | tf_op jit(solution)/shard_map/concatenate | solution.py:38
  38.5 0.0 copy-start.2
  38.5 0.0 copy-start.3
  38.5 0.0 copy-start.1
  38.5 2.4 %reshape.98 = f32[4,1,65536]{2,1,0:T(1,128)} reshape(f32[128,2,16,64]{3,2,1,0:T(8,128)S(1)} %bitcast.60) | data formatting | bytes 2097152
  40.9 4.9 %all-to-all-start.2 = ((f32[4,1,65536]{2,1,0:T(1,128)}), f32[4,1,65536]{2,1,0:T(1,128)S(1)}, u32[]{:S(2)}, u32[]{:S(2)}) async-start(f32[4,1,65536]{2,1,0:T(1,128)} %reshape.98), calls=%async_computation.2 | async-start | bytes 2097152 | tf_op jit(solution)/shard_map/all_to_all | solution.py:39
  45.8 0.0 copy-done.2
  45.8 0.1 dynamic_slice.6
  45.9 0.0 copy-done.3
  45.9 0.1 dynamic_slice.7
  46.0 0.1 broadcast_add_fusion
  46.0 0.0 copy-done.1
  46.0 1.0 %add_divide_fusion = f32[16,32,256]{2,1,0:T(8,128)} fusion(f32[256]{0:T(256)S(1)} %copy-done.1, f32[16,32]{1,0:T(8,128)S(1)} %broadcast_add_fusion), kind=kLoop, calls=%fused_computation.4 | loop fusion | flops 655360 | bytes 527360 | tf_op jit(solution)/shard_map/div | solution.py:46
  47.0 22.3 %all-to-all-done.2 = f32[4,1,65536]{2,1,0:T(1,128)S(1)} async-done(((f32[4,1,65536]{2,1,0:T(1,128)}), f32[4,1,65536]{2,1,0:T(1,128)S(1)}, u32[]{:S(2)}, u32[]{:S(2)}) %all-to-all-start.2) | async-done | bytes 1048608 | tf_op jit(solution)/shard_map/all_to_all | solution.py:39
  69.3 3.7 %reduce.2 = f32[4,65536]{1,0:T(4,128)S(1)} reduce(f32[4,1,65536]{2,1,0:T(1,128)S(1)} %all-to-all-done.2, f32[]{:T(128)} %broadcast.162), dimensions={1}, to_apply=%all_to_all.41.reduce_sub_computation | reduce | bytes 2097156 | tf_op jit(solution)/shard_map/all_to_all | solution.py:39
  72.9 1.0 %reshape.99 = f32[128,2,16,64]{3,2,1,0:T(8,128)S(1)} reshape(f32[4,65536]{1,0:T(4,128)S(1)} %reduce.2) | data formatting | bytes 2097152
  73.9 2.7 %copy.24 = f32[2,16,32,4,64]{4,3,2,1,0:T(4,128)} copy(f32[2,16,32,4,64]{4,1,0,2,3:T(8,128)S(1)} %bitcast.61) | data formatting | bytes 2097152 | tf_op jit(solution)/shard_map/all_to_all | solution.py:39
  76.6 0.0 copy-start
  76.6 2.5 %all_to_all.44 = f32[2,16,32,256]{3,2,1,0:T(8,128)S(1)} reshape(f32[2,16,32,4,64]{4,3,2,1,0:T(4,128)} %copy.24) | data formatting | bytes 2097152 | tf_op jit(solution)/shard_map/all_to_all | solution.py:39
  79.2 0.0 copy-done
  79.2 3.0 %convolution_multiply_fusion = f32[2,16,32,256]{3,2,1,0:T(8,128)} fusion(f32[2,16,32,256]{3,2,1,0:T(8,128)S(1)} %all_to_all.44, f32[16,32,256]{2,1,0:T(8,128)S(1)} %copy-done, s32[256]{0:T(256)S(1)} %multiply_add_fusion), kind=kOutput, calls=%fused_computation | convolution fusion | flops 806551552 | bytes 2622464 | tf_op jit(solution)/shard_map/dot_general | solution.py:18
  (2 shorter events, 0.0 us)
Async XLA Ops:
  4.1 14.9 %all-to-all-start = ((f32[8,1,16384]{2,1,0:T(1,128)}), f32[8,1,16384]{2,1,0:T(1,128)S(1)}, u32[]{:S(2)}, u32[]{:S(2)}) async-start(f32[8,1,16384]{2,1,0:T(1,128)} %reshape.96), calls=%async_computation | async-start | bytes 1048576 | tf_op jit(solution)/shard_map/all_to_all | solution.py:31
  19.0 13.2 %all-to-all-start.1 = ((f32[8,1,16384]{2,1,0:T(1,128)}), f32[8,1,16384]{2,1,0:T(1,128)S(1)}, u32[]{:S(2)}, u32[]{:S(2)}) async-start(f32[8,1,16384]{2,1,0:T(1,128)} %reshape.94), calls=%async_computation.1 | async-start | bytes 1048576 | tf_op jit(solution)/shard_map/all_to_all | solution.py:31
  38.5 7.3 %copy-start.2 = (f32[128]{0:T(128)S(1)}, f32[128]{0:T(128)}, u32[]{:S(2)}) copy-start(f32[128]{0:T(128)} %param.5) | copy-start | bytes 1540
  38.5 7.4 %copy-start.3 = (f32[128]{0:T(128)S(1)}, f32[128]{0:T(128)}, u32[]{:S(2)}) copy-start(f32[128]{0:T(128)} %param.6) | copy-start | bytes 1540
  38.5 7.5 %copy-start.1 = (f32[256]{0:T(256)S(1)}, f32[256]{0:T(256)}, u32[]{:S(2)}) copy-start(f32[256]{0:T(256)} %param.7) | copy-start | bytes 3076
  40.9 28.3 %all-to-all-start.2 = ((f32[4,1,65536]{2,1,0:T(1,128)}), f32[4,1,65536]{2,1,0:T(1,128)S(1)}, u32[]{:S(2)}, u32[]{:S(2)}) async-start(f32[4,1,65536]{2,1,0:T(1,128)} %reshape.98), calls=%async_computation.2 | async-start | bytes 2097152 | tf_op jit(solution)/shard_map/all_to_all | solution.py:39
  76.6 2.5 %copy-start = (f32[16,32,256]{2,1,0:T(8,128)S(1)}, f32[16,32,256]{2,1,0:T(8,128)}, u32[]{:S(2)}) copy-start(f32[16,32,256]{2,1,0:T(8,128)} %add_divide_fusion) | copy-start | bytes 1572868
where the time goes:
time: 82.7 us; the launch traced here: 82.2 us
  waiting for transfers between devices  33.7 us (41%)
  local copies, waits for them, and re-layouts  17.4 us (21%)
  starting transfers between devices  13.7 us (17%)
  matrix products  8.66 us (10%)
  other arithmetic  8.53 us (10%)
    all_to_all x1, waiting for transfers between devices, local(): lax.all_to_all(local_values, 'deep', split_axis=2, concat_axis=3, tiled=T...  22.3 us
    all_to_all x2, waiting for transfers between devices, line_step(): lax.all_to_all(part_values, 'north', split_axis=1, concat_axis=2, tiled=T...  11.4 us
    all_to_all x2, starting transfers between devices, line_step(): lax.all_to_all(part_values, 'north', split_axis=1, concat_axis=2, tiled=T...  8.87 us
    unnamed x14, local copies, waits for them, and re-layouts  7.14 us
    dot_general x3, matrix products, to_modes(): jnp.tensordot(values, transform_table(values.shape[dim]), axes=([dim], [0...  6.88 us
    all_to_all x2, local copies, waits for them, and re-layouts, local(): lax.all_to_all(local_values, 'deep', split_axis=2, concat_axis=3, tiled=T...  5.23 us
    all_to_all x1, starting transfers between devices, local(): lax.all_to_all(local_values, 'deep', split_axis=2, concat_axis=3, tiled=T...  4.88 us
    all_to_all x2, other arithmetic, line_step(): lax.all_to_all(part_values, 'north', split_axis=1, concat_axis=2, tiled=T...  3.74 us
  transfers between devices with their start and end apart: 3, of which 3 were waited for; matrix products, arithmetic and copies ran while one was open for 11% of the time, Pallas kernels for 0%

commit v1 on v0

v1 whole, which is shorter than its diff:
```python
import functools

import jax
import jax.numpy as jnp
import numpy as np
from jax import lax
from jax.experimental import pallas as pl
from jax.experimental.pallas import tpu as pltpu
from jax.sharding import PartitionSpec as P

CHUNKS = 4


def transform_table(count):
    rank = np.arange(count)
    odd = (2 * rank[:, None] + 1) * (2 * rank[None, :] + 1) % (8 * count)
    return (np.cos(np.pi / (4 * count) * odd) * np.sqrt(2.0 / count)).astype(np.float32)


def halves(values):
    high = values.astype(jnp.bfloat16)
    low = (values - high.astype(jnp.float32)).astype(jnp.bfloat16)
    return high, low


def table_halves(table):
    high = table.astype(jnp.bfloat16)
    low = (table - high.astype(np.float32)).astype(jnp.bfloat16)
    return high, low


def partners(me, count):
    found = []
    for step in range(count - 1, 0, -1):
        if count & (count - 1):
            found.append(lax.rem(me + step, count))
            continue
        other = me
        for bit in range(count.bit_length() - 1):
            if step >> bit & 1:
                other = other + (1 - 2 * ((me // 2**bit) % 2)) * 2**bit
        found.append(other)
    return found


def kernel(
    sizes, forcing, hx, hy, hz, sx, sy, sz, out, xin, wa, u, v, r, fac,
    in_sem, ns_sem, nr_sem, ds_sem, dr_sem, own_sem,
):
    north, deep, chunks = sizes
    fields, share_y, share_z, grid_x = forcing.shape
    share_x, part_y = out.shape[1], out.shape[2]
    grid_y, grid_z = v.shape[1], out.shape[3]
    lanes = fields * share_z
    ci = share_x // chunks
    n, d = lax.axis_index("north"), lax.axis_index("deep")
    norths, deeps = partners(n, north), partners(d, deep)

    groups = in_sem.shape[0]
    per = share_y // groups
    loads = []
    for g in range(groups):
        part = (slice(None), pl.ds(g * per, per))
        loads.append(pltpu.make_async_copy(forcing.at[part], xin.at[part], in_sem.at[g]))
        loads[-1].start()
    barrier = pltpu.get_barrier_semaphore()
    for other in norths:
        pl.semaphore_signal(barrier, device_id={"north": other}, device_id_type=pl.DeviceIdType.MESH)
    for other in deeps:
        pl.semaphore_signal(barrier, device_id={"deep": other}, device_id_type=pl.DeviceIdType.MESH)

    pair = 2 if per % 2 == 0 else 1
    for g in range(groups):
        loads[g].wait()
        for y in range(g * per, (g + 1) * per, pair):
            high, low = halves(
                jnp.concatenate([xin[f, y + k] for k in range(pair) for f in range(fields)], axis=0)
            )
            modes = lax.dot_general(
                hx[...],
                jnp.concatenate([high, low, high], axis=1),
                (((1,), (1,)), ((), ())),
                preferred_element_type=jnp.float32,
            )
            for k in range(pair):
                wa[pl.ds(y + k, grid_x, stride=share_y), :] = modes[:, k * lanes : (k + 1) * lanes]

    pl.semaphore_wait(barrier, north + deep - 2)
    block = ci * share_y

    def rows(c, other):
        return pl.ds(pl.multiple_of((c * north + other) * block, block), block)

    def north_copy(c, target, source):
        return pltpu.make_async_remote_copy(
            src_ref=wa.at[rows(c, target)],
            dst_ref=u.at[rows(c, source)],
            send_sem=ns_sem.at[c, target],
            recv_sem=nr_sem.at[c, source],
            device_id={"north": target},
            device_id_type=pl.DeviceIdType.MESH,
        )

    def north_own(c):
        return pltpu.make_async_copy(wa.at[rows(c, n)], u.at[rows(c, n)], own_sem.at[0, c])

    def deep_copy(c, target, source):
        return pltpu.make_async_remote_copy(
            src_ref=v.at[pl.ds(c * ci, ci), pl.ds(pl.multiple_of(target * part_y, part_y), part_y)],
            dst_ref=r.at[source, pl.ds(c * ci, ci)],
            send_sem=ds_sem.at[c, target],
            recv_sem=dr_sem.at[c, source],
            device_id={"deep": target},
            device_id_type=pl.DeviceIdType.MESH,
        )

    def deep_own(c):
        mine = pl.ds(pl.multiple_of(d * part_y, part_y), part_y)
        return pltpu.make_async_copy(
            v.at[pl.ds(c * ci, ci), mine], r.at[d, pl.ds(c * ci, ci)], own_sem.at[1, c]
        )

    for c in range(chunks):
        for other in norths:
            north_copy(c, other, n).start()
        north_own(c).start()

    spot = lax.broadcasted_iota(jnp.int32, (part_y, grid_y), 0) + d * part_y
    along = lax.broadcasted_iota(jnp.int32, (part_y, grid_y), 1)
    column = jnp.sum(jnp.where(spot == along, sy[...], 0.0), axis=1, keepdims=True)
    plane = column + sz[...]
    for i in range(share_x):
        symbol = sx[n * share_x + i] + plane
        fac[pl.ds(i * part_y, part_y), :] = (1.0 - 0.2 * symbol) / (1.0 + 0.2 * symbol)

    pair = 2 if ci % 2 == 0 else 1
    for c in range(chunks):
        for other in norths:
            north_copy(c, n, other).wait_recv()
        north_own(c).wait()
        for i in range(0, ci, pair):
            lines = jnp.concatenate(
                [
                    jnp.concatenate(
                        [
                            u[pl.ds(((c * north + s) * ci + i + k) * share_y, share_y), :]
                            for s in range(north)
                        ],
                        axis=0,
                    )
                    for k in range(pair)
                ],
                axis=1,
            )
            high, low = halves(lines)
            modes = jnp.dot(
                hy[...],
                jnp.concatenate([high, low, high], axis=0),
                preferred_element_type=jnp.float32,
            )
            for k in range(pair):
                v[c * ci + i + k] = modes[:, k * lanes : (k + 1) * lanes]
        for other in deeps:
            deep_copy(c, other, d).start()
        deep_own(c).start()

    for c in range(chunks):
        for other in deeps:
            deep_copy(c, d, other).wait_recv()
        deep_own(c).wait()
        parts = [r[s, pl.ds(c * ci, ci)].reshape(ci * part_y, lanes) for s in range(deep)]
        factor = fac[pl.ds(c * ci * part_y, ci * part_y), :]
        for f in range(fields):
            lines = jnp.concatenate([p[:, f * share_z : (f + 1) * share_z] for p in parts], axis=1)
            high, low = halves(lines)
            modes = jnp.dot(
                jnp.concatenate([high, low, high], axis=1),
                hz[...],
                preferred_element_type=jnp.float32,
            )
            out[f, pl.ds(c * ci, ci)] = (modes * factor).reshape(ci, part_y, grid_z)

    for c in range(chunks):
        for other in norths:
            north_copy(c, other, n).wait_send()
        for other in deeps:
            deep_copy(c, other, d).wait_send()


def local(north, deep, forcing, symbol_x, symbol_y, symbol_z):
    fields, grid_x, share_y, share_z = forcing.shape
    grid_y, grid_z = symbol_y.shape[0], symbol_z.shape[0]
    share_x, part_y = grid_x // north, grid_y // deep
    chunks = CHUNKS if share_x % CHUNKS == 0 else 1
    ci = share_x // chunks
    lanes = fields * share_z

    order = np.arange(grid_x).reshape(north, chunks, ci).transpose(1, 0, 2).reshape(-1)
    high, low = table_halves(transform_table(grid_x)[order])
    hx = np.concatenate([high, high, low], axis=1)
    high, low = table_halves(transform_table(grid_y))
    hy = np.concatenate([high, high, low], axis=1)
    high, low = table_halves(transform_table(grid_z))
    hz = np.concatenate([high, high, low], axis=0)

    groups = 4 if share_y % 4 == 0 else 1
    vmem = pl.BlockSpec(memory_space=pltpu.VMEM)
    return pl.pallas_call(
        functools.partial(kernel, (north, deep, chunks)),
        out_shape=jax.ShapeDtypeStruct((fields, share_x, part_y, grid_z), jnp.float32),
        in_specs=[
            pl.BlockSpec(memory_space=pl.ANY),
            vmem,
            vmem,
            vmem,
            pl.BlockSpec(memory_space=pltpu.SMEM),
            vmem,
            vmem,
        ],
        out_specs=vmem,
        scratch_shapes=[
            pltpu.VMEM((fields, share_y, share_z, grid_x), jnp.float32),
            pltpu.VMEM((grid_x * share_y, lanes), jnp.float32),
            pltpu.VMEM((grid_y * share_x, lanes), jnp.float32),
            pltpu.VMEM((share_x, grid_y, lanes), jnp.float32),
            pltpu.VMEM((deep, share_x, part_y, lanes), jnp.float32),
            pltpu.VMEM((share_x * part_y, grid_z), jnp.float32),
            pltpu.SemaphoreType.DMA((groups,)),
            pltpu.SemaphoreType.DMA((chunks, north)),
            pltpu.SemaphoreType.DMA((chunks, north)),
            pltpu.SemaphoreType.DMA((chunks, deep)),
            pltpu.SemaphoreType.DMA((chunks, deep)),
            pltpu.SemaphoreType.DMA((2, chunks)),
        ],
        compiler_params=pltpu.CompilerParams(collective_id=0, has_side_effects=True),
    )(
        forcing.transpose(0, 2, 3, 1),
        jnp.asarray(hx),
        jnp.asarray(hy),
        jnp.asarray(hz),
        symbol_x,
        symbol_y[None, :],
        symbol_z[None, :],
    )


def solution(mesh):
    placed = (P(None, None, "north", "deep"), P(), P(), P())
    return jax.shard_map(
        functools.partial(local, mesh.shape["north"], mesh.shape["deep"]),
        mesh=mesh,
        in_specs=placed,
        out_specs=P(None, "north", "deep", None),
        check_vma=False,
    )
```

time: 82.7 us -> 41.1 us (0.50)
  Pallas kernels: 0 us -> 38.5 us
  waiting for transfers between devices: 33.7 us -> 0 us
  local copies, waits for them, and re-layouts: 17.4 us -> 2.31 us
  starting transfers between devices: 13.7 us -> 0 us
  matrix products: 8.66 us -> 0 us
  other arithmetic: 8.53 us -> 0 us
    pallas_call x0 -> x1, Pallas kernels: none -> 38.5 us  [local(): pl.pallas_call(functools.partial(kernel, (north, deep, chunks)), out_shap...]
    all_to_all x3 -> x0, waiting for transfers between devices: 33.7 us -> none  [the longest x1 22.3 us: local(): lax.all_to_all(local_values, 'deep', split_axis=2, concat_axis=3, tiled=T...]
    all_to_all x3 -> x0, starting transfers between devices: 13.7 us -> none  [the longest x2 8.87 us: line_step(): lax.all_to_all(part_values, 'north', split_axis=1, concat_axis=2, tiled=T...]
    all_to_all x3 -> x0, other arithmetic: 7.41 us -> none  [the longest x2 3.74 us: line_step(): lax.all_to_all(part_values, 'north', split_axis=1, concat_axis=2, tiled=T...]
    dot_general x3 -> x0, matrix products: 6.88 us -> none  [to_modes(): jnp.tensordot(values, transform_table(values.shape[dim]), axes=([dim], [0...]
    all_to_all x5 -> x0, local copies, waits for them, and re-layouts: 6.03 us -> none  [the longest x2 5.23 us: local(): lax.all_to_all(local_values, 'deep', split_axis=2, concat_axis=3, tiled=T...]
    unnamed x14 -> x1, local copies, waits for them, and re-layouts: 7.14 us -> 2.31 us
    concatenate x1 -> x0, local copies, waits for them, and re-layouts: 1.83 us -> none  [local(): local_values = jnp.concatenate([lower_part, upper_part], axis=0)]
  transfers between devices with their start and end apart: 3 -> 0, of which waited for: 3 -> 0; matrix products, arithmetic and copies ran while one was open for 11% -> 0% of each run, Pallas kernels for 0% -> 0%
where the time goes in v1:
time: 41.1 us; the launch traced here: 40.9 us
  Pallas kernels  38.5 us (94%)
  local copies, waits for them, and re-layouts  2.31 us (6%)
    pallas_call x1, Pallas kernels, local(): pl.pallas_call(functools.partial(kernel, (north, deep, chunks)), out_shap...  38.5 us
    unnamed x1, local copies, waits for them, and re-layouts  2.31 us

profile of v1, /device:TPU:0, one launch (start us, length us, event | category | flops | bytes accessed | tf_op | source)
XLA Modules:
  0.0 40.9 jit_solution(15501928866716850407)
XLA Ops:
  0.0 38.5 %shard_map.73 = f32[2,16,32,256]{3,2,1,0:T(8,128)} custom-call(f32[2,16,64,128]{3,2,1,0:T(8,128)} %bitcast.3, bf16[128,384]{1,0:T(8,128)(2,1)} %constant.6.clone.hx, bf16[128,384]{1,0:T(8,128)(2,1)} %constant.7.clone.hy, bf16[768,256]{1,0:T(8,128)(2,1)} %constant.8.clone.hz, f32[128]{0:T(128)} %sx.1, f32[1,128]{1,0:T(1,128)} %bitcast.5, f32[1,256]{1,0:T(1,128)} %bitcast.4), custom_call_target="tpu_custom_call" | custom-call | tf_op jit(solution)/shard_map/pallas_call | solution.py:208
  38.6 2.3 %copy.9 = f32[2,16,32,256]{3,2,1,0:T(8,128)} copy(f32[2,16,32,256]{3,2,1,0:T(8,128)} %shard_map.73) | data formatting | bytes 2097152

commit v2 on v1

v2 whole, which is shorter than its diff:
```python
import functools
import math

import jax
import jax.numpy as jnp
import numpy as np
from jax import lax
from jax.experimental import pallas as pl
from jax.experimental.pallas import tpu as pltpu
from jax.sharding import PartitionSpec as P

CHUNKS = (2, 4, 6, 4)


def transform_table(count):
    rank = np.arange(count)
    odd = (2 * rank[:, None] + 1) * (2 * rank[None, :] + 1) % (8 * count)
    return (np.cos(np.pi / (4 * count) * odd) * np.sqrt(2.0 / count)).astype(np.float32)


def chunk_starts(share):
    unit = max(1, share // sum(CHUNKS))
    found, start = [], 0
    for weight in CHUNKS:
        size = min(unit * weight, share - start)
        if size > 0:
            found.append((start, size))
        start += size
    if start < share:
        found.append((start, share - start))
    return tuple(found)


def halves(values):
    high = values.astype(jnp.bfloat16)
    low = (values - high.astype(jnp.float32)).astype(jnp.bfloat16)
    return high, low


def table_halves(table):
    high = table.astype(jnp.bfloat16)
    low = (table - high.astype(np.float32)).astype(jnp.bfloat16)
    return high, low


def partners(me, count):
    found = []
    for step in range(count - 1, 0, -1):
        if count & (count - 1):
            found.append(lax.rem(me + step, count))
            continue
        other = me
        for bit in range(count.bit_length() - 1):
            if step >> bit & 1:
                other = other + (1 - 2 * ((me // 2**bit) % 2)) * 2**bit
        found.append(other)
    return found


def kernel(
    sizes, forcing, tx, ty, tz, sx, sy, sz, out, xin, hx, hy, hz, wa, u, v, r, fac,
    in_sem, table_sem, ns_sem, nr_sem, ds_sem, dr_sem, own_sem,
):
    north, deep, chunks = sizes
    fields, share_y, share_z, grid_x = forcing.shape
    share_x, part_y = out.shape[1], out.shape[2]
    grid_y, grid_z = v.shape[1], out.shape[3]
    lanes = fields * share_z
    n, d = lax.axis_index("north"), lax.axis_index("deep")
    norths, deeps = partners(n, north), partners(d, deep)

    barrier = pltpu.get_barrier_semaphore()
    for other in norths:
        pl.semaphore_signal(barrier, device_id={"north": other}, device_id_type=pl.DeviceIdType.MESH)
    for other in deeps:
        pl.semaphore_signal(barrier, device_id={"deep": other}, device_id_type=pl.DeviceIdType.MESH)

    tables = [
        pltpu.make_async_copy(source, target, table_sem.at[k])
        for k, (source, target) in enumerate(((tx, hx), (ty, hy), (tz, hz)))
    ]
    tables[0].start()
    groups = in_sem.shape[0]
    per = share_y // groups
    loads = []
    for g in range(groups):
        part = (slice(None), pl.ds(g * per, per))
        loads.append(pltpu.make_async_copy(forcing.at[part], xin.at[part], in_sem.at[g]))
        loads[-1].start()
    tables[1].start()
    tables[2].start()

    pair = 2 if per % 2 == 0 else 1
    tables[0].wait()
    for g in range(groups):
        loads[g].wait()
        for y in range(g * per, (g + 1) * per, pair):
            high, low = halves(
                jnp.concatenate([xin[f, y + k] for k in range(pair) for f in range(fields)], axis=0)
            )
            modes = lax.dot_general(
                hx[...],
                jnp.concatenate([high, low, high], axis=1),
                (((1,), (1,)), ((), ())),
                preferred_element_type=jnp.float32,
            )
            for k in range(pair):
                wa[pl.ds(y + k, grid_x, stride=share_y), :] = modes[:, k * lanes : (k + 1) * lanes]

    pl.semaphore_wait(barrier, north + deep - 2)

    def rows(c, other):
        start, size = chunks[c]
        at = (start * north + other * size) * share_y
        return pl.ds(pl.multiple_of(at, share_y), size * share_y)

    def north_copy(c, target, source):
        return pltpu.make_async_remote_copy(
            src_ref=wa.at[rows(c, target)],
            dst_ref=u.at[rows(c, source)],
            send_sem=ns_sem.at[c, target],
            recv_sem=nr_sem.at[c, source],
            device_id={"north": target},
            device_id_type=pl.DeviceIdType.MESH,
        )

    def north_own(c):
        return pltpu.make_async_copy(wa.at[rows(c, n)], u.at[rows(c, n)], own_sem.at[0, c])

    def deep_copy(c, target, source):
        return pltpu.make_async_remote_copy(
            src_ref=v.at[pl.ds(*chunks[c]), pl.ds(pl.multiple_of(target * part_y, part_y), part_y)],
            dst_ref=r.at[source, pl.ds(*chunks[c])],
            send_sem=ds_sem.at[c, target],
            recv_sem=dr_sem.at[c, source],
            device_id={"deep": target},
            device_id_type=pl.DeviceIdType.MESH,
        )

    def deep_own(c):
        mine = pl.ds(pl.multiple_of(d * part_y, part_y), part_y)
        return pltpu.make_async_copy(
            v.at[pl.ds(*chunks[c]), mine], r.at[d, pl.ds(*chunks[c])], own_sem.at[1, c]
        )

    for c in range(len(chunks)):
        for other in norths:
            north_copy(c, other, n).start()
        north_own(c).start()

    spot = lax.broadcasted_iota(jnp.int32, (part_y, grid_y), 0) + d * part_y
    along = lax.broadcasted_iota(jnp.int32, (part_y, grid_y), 1)
    column = jnp.sum(jnp.where(spot == along, sy[...], 0.0), axis=1, keepdims=True)
    plane = column + sz[...]
    for i in range(share_x):
        symbol = sx[n * share_x + i] + plane
        fac[pl.ds(i * part_y, part_y), :] = (1.0 - 0.2 * symbol) / (1.0 + 0.2 * symbol)

    tables[1].wait()
    for c in range(len(chunks)):
        for other in norths:
            north_copy(c, n, other).wait_recv()
        north_own(c).wait()
        start, size = chunks[c]
        for i in range(0, size, 2):
            pair = min(2, size - i)
            lines = jnp.concatenate(
                [
                    jnp.concatenate(
                        [
                            u[pl.ds((start * north + s * size + i + k) * share_y, share_y), :]
                            for s in range(north)
                        ],
                        axis=0,
                    )
                    for k in range(pair)
                ],
                axis=1,
            )
            high, low = halves(lines)
            modes = jnp.dot(
                hy[...],
                jnp.concatenate([high, low, high], axis=0),
                preferred_element_type=jnp.float32,
            )
            for k in range(pair):
                v[start + i + k] = modes[:, k * lanes : (k + 1) * lanes]
        for other in deeps:
            deep_copy(c, other, d).start()
        deep_own(c).start()

    tables[2].wait()
    for c in range(len(chunks)):
        start, size = chunks[c]
        for other in deeps:
            deep_copy(c, d, other).wait_recv()
        deep_own(c).wait()
        parts = [r[s, pl.ds(*chunks[c])].reshape(size * part_y, lanes) for s in range(deep)]
        factor = fac[pl.ds(start * part_y, size * part_y), :]
        for f in range(fields):
            lines = jnp.concatenate([p[:, f * share_z : (f + 1) * share_z] for p in parts], axis=1)
            high, low = halves(lines)
            modes = jnp.dot(
                jnp.concatenate([high, low, high], axis=1),
                hz[...],
                preferred_element_type=jnp.float32,
            )
            out[f, pl.ds(*chunks[c])] = (modes * factor).reshape(size, part_y, grid_z)

    for c in range(len(chunks)):
        for other in norths:
            north_copy(c, other, n).wait_send()
        for other in deeps:
            deep_copy(c, other, d).wait_send()


def local(north, deep, forcing, symbol_x, symbol_y, symbol_z):
    fields, grid_x, share_y, share_z = forcing.shape
    grid_y, grid_z = symbol_y.shape[0], symbol_z.shape[0]
    share_x, part_y = grid_x // north, grid_y // deep
    chunks = chunk_starts(share_x)
    lanes = fields * share_z

    modes = np.arange(grid_x).reshape(north, share_x)
    order = np.concatenate([modes[:, start : start + size].reshape(-1) for start, size in chunks])
    high, low = table_halves(transform_table(grid_x)[order])
    hx = np.concatenate([high, high, low], axis=1)
    high, low = table_halves(transform_table(grid_y))
    hy = np.concatenate([high, high, low], axis=1)
    high, low = table_halves(transform_table(grid_z))
    hz = np.concatenate([high, high, low], axis=0)

    groups = share_y // 4 if share_y % 4 == 0 else 1
    vmem = pl.BlockSpec(memory_space=pltpu.VMEM)
    buffers = [
        pltpu.VMEM((fields, share_y, share_z, grid_x), jnp.float32),
        pltpu.VMEM(hx.shape, jnp.bfloat16),
        pltpu.VMEM(hy.shape, jnp.bfloat16),
        pltpu.VMEM(hz.shape, jnp.bfloat16),
        pltpu.VMEM((grid_x * share_y, lanes), jnp.float32),
        pltpu.VMEM((grid_y * share_x, lanes), jnp.float32),
        pltpu.VMEM((share_x, grid_y, lanes), jnp.float32),
        pltpu.VMEM((deep, share_x, part_y, lanes), jnp.float32),
        pltpu.VMEM((share_x * part_y, grid_z), jnp.float32),
    ]
    result = fields * share_x * part_y * grid_z
    held = sum(math.prod(b.shape) * jnp.dtype(b.dtype).itemsize for b in buffers)
    return pl.pallas_call(
        functools.partial(kernel, (north, deep, chunks)),
        out_shape=pltpu.VMEM((fields, share_x, part_y, grid_z), jnp.float32),
        in_specs=[
            pl.BlockSpec(memory_space=pltpu.HBM),
            pl.BlockSpec(memory_space=pltpu.HBM),
            pl.BlockSpec(memory_space=pltpu.HBM),
            pl.BlockSpec(memory_space=pltpu.HBM),
            pl.BlockSpec(memory_space=pltpu.SMEM),
            vmem,
            vmem,
        ],
        out_specs=vmem,
        scratch_shapes=[
            *buffers,
            pltpu.SemaphoreType.DMA((groups,)),
            pltpu.SemaphoreType.DMA((3,)),
            pltpu.SemaphoreType.DMA((len(chunks), north)),
            pltpu.SemaphoreType.DMA((len(chunks), north)),
            pltpu.SemaphoreType.DMA((len(chunks), deep)),
            pltpu.SemaphoreType.DMA((len(chunks), deep)),
            pltpu.SemaphoreType.DMA((2, len(chunks))),
        ],
        compiler_params=pltpu.CompilerParams(
            collective_id=0, has_side_effects=True, vmem_limit_bytes=max(held + 2**23, 60 * 2**20 - 4 * result)
        ),
    )(
        forcing.transpose(0, 2, 3, 1),
        jnp.asarray(hx),
        jnp.asarray(hy),
        jnp.asarray(hz),
        symbol_x,
        symbol_y[None, :],
        symbol_z[None, :],
    )


def solution(mesh):
    placed = (P(None, None, "north", "deep"), P(), P(), P())
    return jax.shard_map(
        functools.partial(local, mesh.shape["north"], mesh.shape["deep"]),
        mesh=mesh,
        in_specs=placed,
        out_specs=P(None, "north", "deep", None),
        check_vma=False,
    )
```

time: 41.1 us -> 38 us (0.925)
  Pallas kernels: 38.5 us -> 36.9 us
  local copies, waits for them, and re-layouts: 2.31 us -> 0.97 us
    pallas_call x1, Pallas kernels: 38.5 us -> 36.9 us  [local(): pl.pallas_call(functools.partial(kernel, (north, deep, chunks)), out_shap...]
    unnamed x1, local copies, waits for them, and re-layouts: 2.31 us -> 0.97 us
where the time goes in v2:
time: 38 us; the launch traced here: 37.8 us
  Pallas kernels  36.9 us (97%)
  local copies, waits for them, and re-layouts  0.97 us (3%)
    pallas_call x1, Pallas kernels, local(): pl.pallas_call(functools.partial(kernel, (north, deep, chunks)), out_shap...  36.9 us
    unnamed x1, local copies, waits for them, and re-layouts  0.97 us

profile of v2, /device:TPU:0, one launch (start us, length us, event | category | flops | bytes accessed | tf_op | source)
XLA Modules:
  0.0 37.8 jit_solution(6653647218080676000)
XLA Ops:
  0.0 36.9 %shard_map.73 = f32[2,16,32,256]{3,2,1,0:T(8,128)S(1)} custom-call(f32[2,16,64,128]{3,2,1,0:T(8,128)} %bitcast.3, bf16[128,384]{1,0:T(8,128)(2,1)} %constant.6.clone.tx, bf16[128,384]{1,0:T(8,128)(2,1)} %constant.7.clone.ty, bf16[768,256]{1,0:T(8,128)(2,1)} %constant.8.clone.tz, f32[128]{0:T(128)} %sx.1, f32[1,128]{1,0:T(1,128)} %bitcast.5, f32[1,256]{1,0:T(1,128)} %bitcast.4), custom_call_target="tpu_custom_call" | custom-call | tf_op jit(solution)/shard_map/pallas_call | solution.py:248
  36.9 1.0 %copy.9 = f32[2,16,32,256]{3,2,1,0:T(8,128)} copy(f32[2,16,32,256]{3,2,1,0:T(8,128)S(1)} %shard_map.73) | data formatting | bytes 2097152

commit v3 on v2

--- a/solution.py
+++ b/solution.py
@@ -58,7 +58,7 @@
 
 
 def kernel(
-    sizes, forcing, tx, ty, tz, sx, sy, sz, out, xin, hx, hy, hz, wa, u, v, r, fac,
+    sizes, forcing, tx, ty, tz, gx, gy, gz, out, sx, sy, sz, xin, hx, hy, hz, wa, u, v, r, fac,
     in_sem, table_sem, ns_sem, nr_sem, ds_sem, dr_sem, own_sem,
 ):
     north, deep, chunks = sizes
@@ -77,7 +77,7 @@
 
     tables = [
         pltpu.make_async_copy(source, target, table_sem.at[k])
-        for k, (source, target) in enumerate(((tx, hx), (ty, hy), (tz, hz)))
+        for k, (source, target) in enumerate(((tx, hx), (ty, hy), (tz, hz), (gx, sx), (gy, sy), (gz, sz)))
     ]
     tables[0].start()
     groups = in_sem.shape[0]
@@ -87,8 +87,8 @@
         part = (slice(None), pl.ds(g * per, per))
         loads.append(pltpu.make_async_copy(forcing.at[part], xin.at[part], in_sem.at[g]))
         loads[-1].start()
-    tables[1].start()
-    tables[2].start()
+    for table in tables[1:]:
+        table.start()
 
     pair = 2 if per % 2 == 0 else 1
     tables[0].wait()
@@ -148,12 +148,17 @@
             north_copy(c, other, n).start()
         north_own(c).start()
 
+    for table in tables[3:]:
+        table.wait()
     spot = lax.broadcasted_iota(jnp.int32, (part_y, grid_y), 0) + d * part_y
     along = lax.broadcasted_iota(jnp.int32, (part_y, grid_y), 1)
     column = jnp.sum(jnp.where(spot == along, sy[...], 0.0), axis=1, keepdims=True)
     plane = column + sz[...]
+    spot = lax.broadcasted_iota(jnp.int32, (share_x, sx.shape[1]), 0) + n * share_x
+    along = lax.broadcasted_iota(jnp.int32, (share_x, sx.shape[1]), 1)
+    column = jnp.sum(jnp.where(spot == along, sx[...], 0.0), axis=1, keepdims=True)
     for i in range(share_x):
-        symbol = sx[n * share_x + i] + plane
+        symbol = column[i : i + 1] + plane
         fac[pl.ds(i * part_y, part_y), :] = (1.0 - 0.2 * symbol) / (1.0 + 0.2 * symbol)
 
     tables[1].wait()
@@ -248,20 +253,15 @@
     return pl.pallas_call(
         functools.partial(kernel, (north, deep, chunks)),
         out_shape=pltpu.VMEM((fields, share_x, part_y, grid_z), jnp.float32),
-        in_specs=[
-            pl.BlockSpec(memory_space=pltpu.HBM),
-            pl.BlockSpec(memory_space=pltpu.HBM),
-            pl.BlockSpec(memory_space=pltpu.HBM),
-            pl.BlockSpec(memory_space=pltpu.HBM),
-            pl.BlockSpec(memory_space=pltpu.SMEM),
-            vmem,
-            vmem,
-        ],
+        in_specs=[pl.BlockSpec(memory_space=pltpu.HBM)] * 7,
         out_specs=vmem,
         scratch_shapes=[
+            pltpu.VMEM((1, grid_x), jnp.float32),
+            pltpu.VMEM((1, grid_y), jnp.float32),
+            pltpu.VMEM((1, grid_z), jnp.float32),
             *buffers,
             pltpu.SemaphoreType.DMA((groups,)),
-            pltpu.SemaphoreType.DMA((3,)),
+            pltpu.SemaphoreType.DMA((6,)),
             pltpu.SemaphoreType.DMA((len(chunks), north)),
             pltpu.SemaphoreType.DMA((len(chunks), north)),
             pltpu.SemaphoreType.DMA((len(chunks), deep)),
@@ -276,7 +276,7 @@
         jnp.asarray(hx),
         jnp.asarray(hy),
         jnp.asarray(hz),
-        symbol_x,
+        symbol_x[None, :],
         symbol_y[None, :],
         symbol_z[None, :],
     )

time: 38 us -> 37.3 us (0.982)
  Pallas kernels: 36.9 us -> 36.2 us
    pallas_call x1, Pallas kernels: 36.9 us -> 36.2 us  [local(): pl.pallas_call(functools.partial(kernel, (north, deep, chunks)), out_shap...]
where the time goes in v3:
time: 37.3 us; the launch traced here: 37.1 us
  Pallas kernels  36.2 us (97%)
  local copies, waits for them, and re-layouts  0.97 us (3%)
    pallas_call x1, Pallas kernels, local(): pl.pallas_call(functools.partial(kernel, (north, deep, chunks)), out_shap...  36.2 us
    unnamed x1, local copies, waits for them, and re-layouts  0.97 us

profile of v3, /device:TPU:0, one launch (start us, length us, event | category | flops | bytes accessed | tf_op | source)
XLA Modules:
  0.0 37.1 jit_solution(16016604204722244724)
XLA Ops:
  0.0 36.2 %shard_map.73 = f32[2,16,32,256]{3,2,1,0:T(8,128)S(1)} custom-call(f32[2,16,64,128]{3,2,1,0:T(8,128)} %bitcast.4, bf16[128,384]{1,0:T(8,128)(2,1)} %constant.6.clone.tx, bf16[128,384]{1,0:T(8,128)(2,1)} %constant.7.clone.ty, bf16[768,256]{1,0:T(8,128)(2,1)} %constant.8.clone.tz, f32[1,128]{1,0:T(1,128)} %bitcast.6, f32[1,128]{1,0:T(1,128)} %bitcast.7, ...), custom_call_target="tpu_custom_call" | custom-call | tf_op jit(solution)/shard_map/pallas_call | solution.py:253
  36.2 1.0 %copy.9 = f32[2,16,32,256]{3,2,1,0:T(8,128)} copy(f32[2,16,32,256]{3,2,1,0:T(8,128)S(1)} %shard_map.73) | data formatting | bytes 2097152

commit v4 on v3

--- a/solution.py
+++ b/solution.py
@@ -68,6 +68,7 @@
     lanes = fields * share_z
     n, d = lax.axis_index("north"), lax.axis_index("deep")
     norths, deeps = partners(n, north), partners(d, deep)
+    deeps = deeps[1:] + deeps[:1]
 
     barrier = pltpu.get_barrier_semaphore()
     for other in norths:

time: 37.3 us -> 36.3 us (0.973)
  Pallas kernels: 36.2 us -> 35.2 us
    pallas_call x1, Pallas kernels: 36.2 us -> 35.2 us  [local(): pl.pallas_call(functools.partial(kernel, (north, deep, chunks)), out_shap...]
where the time goes in v4:
time: 36.3 us; the launch traced here: 36.2 us
  Pallas kernels  35.2 us (97%)
  local copies, waits for them, and re-layouts  0.97 us (3%)
    pallas_call x1, Pallas kernels, local(): pl.pallas_call(functools.partial(kernel, (north, deep, chunks)), out_shap...  35.2 us
    unnamed x1, local copies, waits for them, and re-layouts  0.97 us

profile of v4, /device:TPU:0, one launch (start us, length us, event | category | flops | bytes accessed | tf_op | source)
XLA Modules:
  0.0 36.2 jit_solution(6066154667070678306)
XLA Ops:
  0.0 35.2 %shard_map.73 = f32[2,16,32,256]{3,2,1,0:T(8,128)S(1)} custom-call(f32[2,16,64,128]{3,2,1,0:T(8,128)} %bitcast.4, bf16[128,384]{1,0:T(8,128)(2,1)} %constant.6.clone.tx, bf16[128,384]{1,0:T(8,128)(2,1)} %constant.7.clone.ty, bf16[768,256]{1,0:T(8,128)(2,1)} %constant.8.clone.tz, f32[1,128]{1,0:T(1,128)} %bitcast.6, f32[1,128]{1,0:T(1,128)} %bitcast.7, ...), custom_call_target="tpu_custom_call" | custom-call | tf_op jit(solution)/shard_map/pallas_call | solution.py:254
  35.2 1.0 %copy.9 = f32[2,16,32,256]{3,2,1,0:T(8,128)} copy(f32[2,16,32,256]{3,2,1,0:T(8,128)S(1)} %shard_map.73) | data formatting | bytes 2097152
